TPU v7x, 8 devices: a whole 2x2x1 slice. The times are simulated.
8 devices in a mesh: pod: 1 (over z), data: 2 (over y), stage: 4 (over x, core).
Axes of the slice: x: 2, y: 2, z: 1, core: 2. Of those that a mesh axis runs over, the one named last changes fastest.
Arguments:
- x_last: bfloat16 [4096, 2560], P(('pod', 'data', 'stage'))
- w_head: bfloat16 [51200, 2560], P('stage')
- labels: int32 [4096], P(('pod', 'data'))
- loss_mask: int32 [4096], P(('pod', 'data'))
- w_embed: bfloat16 [51200, 2560], P('stage')
- tok_ids: int32 [4096], P(('pod', 'data'))
- act_in: bfloat16 [16384, 2560], P(('pod', 'data', 'stage'))
- w_up: bfloat16 [4, 2560, 10240], P('stage')
- w_down: bfloat16 [4, 10240, 2560], P('stage')
Outputs:
- output 1: float32 [1], P('pod')
- output 2: float32 [4096, 2560], P(('pod', 'data', 'stage'))
- output 3: bfloat16 [51200, 2560], P(('pod', 'stage'))
- output 4: bfloat16 [4096, 2560], P(('pod', 'data', 'stage'))
- output 5: bfloat16 [16384, 2560], P(('pod', 'data', 'stage'))
All inputs are finite; a program needn't handle non-finite values.
Results may differ from a plain program's by a relative error of at most 0.001.
Values are sent between devices in bfloat16 or wider.
A program may use at most 1.25 GiB of HBM per device.

v0:
```python
import jax
import jax.numpy as jnp
from jax import lax
from jax.sharding import PartitionSpec as P


def solution(mesh):
    n_data = mesh.shape['data']
    tok_spec = P(('pod', 'data', 'stage'), None)
    rep_spec = P(('pod', 'data'))
    vocab_spec = P('stage', None)
    layer_spec = P('stage', None, None)

    def local_step(x_rows, w_head, labels, loss_mask, w_embed, tok_ids, act_in, w_up, w_down):
        stage_idx = lax.axis_index('stage')
        slice_rows = w_head.shape[0]
        offset = stage_idx * slice_rows
        x_full = lax.all_gather(x_rows, 'stage', axis=0, tiled=True)
        logits = jnp.einsum('td,vd->tv', x_full, w_head, preferred_element_type=jnp.float32)
        loc_max = jnp.max(logits, axis=1)
        shifted = jnp.exp(logits - loc_max[:, None])
        loc_sum = jnp.sum(shifted, axis=1)
        col_ids = lax.broadcasted_iota(jnp.int32, (1, slice_rows), 1) + offset
        is_label = labels[:, None] == col_ids
        loc_target = jnp.sum(jnp.where(is_label, logits, 0.0), axis=1)
        glob_max = lax.pmax(loc_max, 'stage')
        rescale = jnp.exp(loc_max - glob_max)
        stat_sums = lax.psum(jnp.stack([loc_sum * rescale, loc_target]), 'stage')
        total_sum = stat_sums[0]
        target = stat_sums[1]
        weights = loss_mask.astype(jnp.float32)
        loss_denom = jnp.maximum(jnp.sum(weights), 1.0)
        rep_loss = jnp.sum(weights * (jnp.log(total_sum) + glob_max - target)) / loss_denom
        mean_loss = lax.psum(rep_loss, 'data') / n_data
        soft_probs = shifted * (rescale / total_sum)[:, None]
        row_scale = (weights / loss_denom)[:, None]
        grad_logits = (jnp.where(is_label, soft_probs - 1.0, soft_probs) * row_scale).astype(jnp.bfloat16)
        dx_part = jnp.dot(grad_logits, w_head, preferred_element_type=jnp.float32)
        grad_x = lax.psum_scatter(dx_part, 'stage', scatter_dimension=0, tiled=True)
        dw_part = jnp.einsum('tv,td->vd', grad_logits, x_full, preferred_element_type=jnp.float32)
        grad_head = (lax.psum(dw_part, 'data') / n_data).astype(jnp.bfloat16)
        local_ids = tok_ids - offset
        in_slice = (local_ids >= 0) & (local_ids < slice_rows)
        rows_emb = jnp.take(w_embed, jnp.clip(local_ids, 0, slice_rows - 1), axis=0)
        emb_part = jnp.where(in_slice[:, None], rows_emb, jnp.zeros_like(rows_emb))
        embed_out = lax.psum_scatter(emb_part, 'stage', scatter_dimension=0, tiled=True)
        hidden = jax.nn.gelu(jnp.dot(act_in, w_up[0], preferred_element_type=jnp.float32)).astype(jnp.bfloat16)
        mlp_f32 = act_in.astype(jnp.float32) + jnp.dot(hidden, w_down[0], preferred_element_type=jnp.float32)
        return mean_loss.reshape(1), grad_x, grad_head, embed_out, mlp_f32.astype(jnp.bfloat16)

    return jax.shard_map(local_step, mesh=mesh, in_specs=(tok_spec, vocab_spec, rep_spec, rep_spec, vocab_spec, rep_spec, tok_spec, layer_spec, layer_spec), out_specs=(P('pod'), tok_spec, P(('pod', 'stage'), None), tok_spec, tok_spec), check_vma=False)
```

profile of v0, /device:TPU:0, one launch (start us, length us, event | category | flops | bytes accessed | tf_op | source)
XLA Modules:
  0.0 3559.2 jit_solution(5669673766487767131)
XLA Ops:
  7.2 0.7 all-gather.2.cloned.1.call-update
  7.9 0.0 all-reduce.2.cloned.1.call-start
  8.0 0.6 iota_add_fusion
  8.6 71.6 %all-gather.2.cloned.1.call-done = bf16[2048,2560]{1,0:T(8,128)(2,1)} async-done(((bf16[512,2560]{1,0:T(8,128)(2,1)}), bf16[2048,2560]{1,0:T(8,128)(2,1)}) %all-gather.2.cloned.1.call-update) | async-done | bytes 10485776 | tf_op jit(solution)/shard_map/all_gather | solution.py:18
  80.2 149.5 %fusion.38 = (f32[2048]{0:T(1024)S(1)}, f32[2048,12800]{1,0:T(8,128)}) fusion(bf16[2048,2560]{1,0:T(8,128)(2,1)} %all-gather.2.cloned.1.call-done, bf16[12800,2560]{1,0:T(8,128)(2,1)} %param.10), kind=kOutput, calls=%fused_computation.44 | convolution fusion | flops 134243942400 | bytes 180887552 | tf_op jit(solution)/shard_map/td,vd->tv/dot_general | solution.py:19
  229.7 6.2 pmax.7
  235.9 35.0 fusion.3
  271.0 10.1 psum.21
  281.2 0.6 convert_reduce_fusion
  282.4 50.9 %fusion.2 = bf16[2048,12800]{1,0:T(8,128)(2,1)} fusion(f32[2048,12800]{1,0:T(8,128)} %get-tuple-element.15, f32[2048]{0:T(1024)S(1)} %convert_divide_fusion, f32[2048]{0:T(1024)S(1)} %get-tuple-element.9, s32[12800]{0:T(1024)S(1)} %copy-done, f32[2048]{0:T(1024)S(1)} %get-tuple-element.14, s32[2048]{0:T(1024)S(1)} %copy-done.1), kind=kLoop, calls=%fused_computation.7 | loop fusion | flops 183500800 | bytes 157370368 | tf_op jit(solution)/shard_map/convert_element_type | solution.py:37
  333.4 158.2 %fusion.40 = f32[12800,2560]{1,0:T(8,128)} fusion(bf16[2048,12800]{1,0:T(8,128)(2,1)} %fusion.2, bf16[2048,2560]{1,0:T(8,128)(2,1)} %all-gather.2.cloned.1.call-done), kind=kOutput, calls=%fused_computation.46 | convolution fusion | flops 134217728000 | bytes 193986560 | tf_op jit(solution)/shard_map/tv,td->vd/dot_general | solution.py:40
  491.6 0.0 reduce-scatter.5.cloned.1.call-start
  491.7 0.6 copy-done.3
  492.3 98.3 %gather_fusion = bf16[2048,2560]{1,0:T(8,128)(2,1)} fusion(bf16[12800,2560]{1,0:T(8,128)(2,1)} %param.13, s32[2048]{0:T(1024)S(1)} %fusion.30), kind=kCustom, calls=%fused_computation | custom fusion | bytes 20979712 | tf_op jit(solution)/shard_map/jit(_take)/gather | solution.py:44
  590.6 10.6 select_select_fusion
  601.2 0.0 reduce-scatter.3.cloned.1.call-start
  601.3 136.5 %fusion.57 = bf16[2048,10240]{1,0:T(8,128)(2,1)} fusion(bf16[2048,2560]{1,0:T(8,128)(2,1)} %param.15, bf16[1,2560,10240]{2,1,0:T(8,128)(2,1)} %param.16), kind=kOutput, calls=%fused_computation.17.clone.clone.clone.clone.1 | convolution fusion | flops 107562926080 | bytes 104857600 | tf_op jit(solution)/shard_map/dot_general | solution.py:47
  738.5 148.4 %fusion.39 = f32[2048,2560]{1,0:T(8,128)} fusion(bf16[2048,12800]{1,0:T(8,128)(2,1)} %fusion.2, bf16[12800,2560]{1,0:T(8,128)(2,1)} %param.10), kind=kOutput, calls=%fused_computation.45 | convolution fusion | flops 134217728000 | bytes 138936320 | tf_op jit(solution)/shard_map/dot_general | solution.py:38
  886.9 121.7 %add_convert_fusion = bf16[2048,2560]{1,0:T(8,128)(2,1)} fusion(bf16[2048,2560]{1,0:T(8,128)(2,1)} %param.15, bf16[1,10240,2560]{2,1,0:T(8,128)(2,1)} %param.17, bf16[2048,10240]{1,0:T(8,128)(2,1)} %fusion.57), kind=kOutput, calls=%fused_computation.25 | convolution fusion | flops 107389911040 | bytes 115343360 | tf_op jit(solution)/shard_map/dot_general | solution.py:48
  1008.6 5.5 psum.22
  1014.8 2306.1 %all-reduce.2.cloned.1.call-done = f32[12800,2560]{1,0:T(8,128)} async-done(((f32[12800,2560]{1,0:T(8,128)}), f32[12800,2560]{1,0:T(8,128)}) %all-reduce.2.cloned.1.call-update) | async-done | bytes 131072016 | tf_op jit(solution)/shard_map/psum | solution.py:41
  3320.8 62.1 %multiply_convert_fusion = bf16[12800,2560]{1,0:T(8,128)(2,1)} fusion(f32[12800,2560]{1,0:T(8,128)} %all-reduce.2.cloned.1.call-done), kind=kLoop, calls=%fused_computation.3 | loop fusion | flops 65536000 | bytes 196608000 | tf_op jit(solution)/shard_map/convert_element_type | solution.py:41
  3383.0 21.2 reduce-scatter.5.cloned.1.call-done
  3404.1 147.0 %reduce-scatter.3.cloned.1.call-done = f32[512,2560]{1,0:T(8,128)} async-done(((f32[2048,2560]{1,0:T(8,128)}), f32[512,2560]{1,0:T(8,128)}) %reduce-scatter.3.cloned.1.call-update) | async-done | bytes 5242896 | tf_op jit(solution)/shard_map/reduce_scatter | solution.py:39
  (17 shorter events, 0.2 us)
Async XLA Ops:
  7.2 73.0 %all-gather.2.cloned.1.call-start = ((), (), s32[]{:S(2)}) async-start(), calls=%async_computation.2 | async-start | bytes 13107200 | tf_op jit(solution)/shard_map/all_gather | solution.py:18
  7.9 3312.9 %all-reduce.2.cloned.1.call-start = ((), (), s32[]{:S(2)}) async-start(), calls=%async_computation.4 | async-start | bytes 262144000 | tf_op jit(solution)/shard_map/psum | solution.py:41
  80.2 155.7 %copy-start = (s32[12800]{0:T(1024)S(1)}, s32[12800]{0:T(1024)}, u32[]{:S(2)}) copy-start(s32[12800]{0:T(1024)} %iota_add_fusion) | copy-start | bytes 153604
  80.2 155.7 %copy-start.1 = (s32[2048]{0:T(1024)S(1)}, s32[2048]{0:T(1024)}, u32[]{:S(2)}) copy-start(s32[2048]{0:T(1024)} %param.11) | copy-start | bytes 24580
  235.9 45.2 %copy-start.2 = (s32[2048]{0:T(1024)S(1)}, s32[2048]{0:T(1024)}, u32[]{:S(2)}) copy-start(s32[2048]{0:T(1024)} %param.12) | copy-start | bytes 24580
  491.6 0.7 copy-start.3
  491.6 2912.5 %reduce-scatter.5.cloned.1.call-start = ((), (), s32[]{:S(2)}) async-start(), calls=%async_computation.5 | async-start | bytes 13107200 | tf_op jit(solution)/shard_map/reduce_scatter | solution.py:46
  601.2 2949.9 %reduce-scatter.3.cloned.1.call-start = ((), (), s32[]{:S(2)}) async-start(), calls=%async_computation.3 | async-start | bytes 26214400 | tf_op jit(solution)/shard_map/reduce_scatter | solution.py:39
Sparse Core Ops, SparseCore 0:
  9.5 70.6 all-gather.1
  491.7 2829.0 all-reduce.1
  3324.0 80.1 reduce-scatter.4
  3407.1 143.9 reduce-scatter.2
where the time goes:
time: 3570 us; the launch traced here: 3560 us
  waiting for transfers between devices  2550 us (71%)
  matrix products  714 us (20%)
  other arithmetic  160 us (4%)
  local copies, waits for them, and re-layouts  98.9 us (3%)
    psum x1, waiting for transfers between devices, local_step(): grad_head = (lax.psum(dw_part, 'data') / n_data).astype(jnp.bfloat16)  2310 us
    dot_general x1, matrix products, local_step(): jnp.einsum('tv,td->vd', grad_logits, x_full, preferred_element_type=jnp.f...  158 us
    dot_general x1, matrix products, local_step(): jnp.einsum('td,vd->tv', x_full, w_head, preferred_element_type=jnp.float32)  149 us
    dot_general x1, matrix products, local_step(): dx_part = jnp.dot(grad_logits, w_head, preferred_element_type=jnp.float32)  148 us
    reduce_scatter x1, waiting for transfers between devices, local_step(): grad_x = lax.psum_scatter(dx_part, 'stage', scatter_dimension=0, tiled=True)  147 us
    dot_general x1, matrix products, local_step(): jnp.dot(act_in, w_up[0], preferred_element_type=jnp.float32)  137 us
    dot_general x1, matrix products, local_step(): jnp.dot(hidden, w_down[0], preferred_element_type=jnp.float32)  122 us
    gather x1, local copies, waits for them, and re-layouts, local_step(): rows_emb = jnp.take(w_embed, jnp.clip(local_ids, 0, slice_rows - 1), axis=0)  98.3 us
  transfers between devices with their start and end apart: 4, of which 4 were waited for; matrix products, arithmetic and copies ran while one was open for 16% of the time, Pallas kernels for 0%

commit v1 on v0

v1 whole, which is shorter than its diff:
```python
import functools

import jax
import jax.numpy as jnp
from jax import lax
from jax.experimental import pallas as pl
from jax.experimental.pallas import tpu as pltpu
from jax.sharding import PartitionSpec as P


BF = jnp.bfloat16
F32 = jnp.float32
V = 12800
D = 2560
FF = 10240
TB = 512
PAIR = 2 * TB
ALL = 4 * TB
CB = 512
BV = 512
NT = V // BV
SUB = 8
A = 11
NR = NT - 2 * A
CALLS = ((0, (1,)), (0, (3,)), (NR, (4, 3)))
EG = 64
LANES = 2 * EG

VM = pl.BlockSpec(memory_space=pltpu.VMEM)
ANY = pl.BlockSpec(memory_space=pl.ANY)


def cdot(a, b, ca, cb):
    return lax.dot_general(a, b, (((ca,), (cb,)), ((), ())), preferred_element_type=F32)


def tree(f, xs):
    while len(xs) > 1:
        xs = [f(xs[i], xs[i + 1]) if i + 1 < len(xs) else xs[i] for i in range(0, len(xs), 2)]
    return xs[0]


def cols(k, n=TB):
    return slice(k * n, k * n + n)


def row(ref, i, c=slice(None)):
    return ref[i:i + 1, c]


def rows_at(ref, start, n):
    return ref.at[pl.ds(pl.multiple_of(start, n), n)]


def copy_all(cps):
    for c in cps:
        c.start()
    for c in cps:
        c.wait()


def params(mib=62, **kw):
    return pltpu.CompilerParams(vmem_limit_bytes=mib * 2**20, **kw)


def cost(flops, nbytes):
    return pl.CostEstimate(flops=int(flops), bytes_accessed=int(nbytes), transcendentals=0)


HEAD_COST = cost(2 * V * PAIR * D, V * D * 2 + V * PAIR * 4)


def z_body(k0, npre, *refs):
    xa_ref, xb_ref, lab_ref, w_ref = refs[:4]
    z_hbm, st_ref, m_s, s_s, t_s, zs, sem = refs[4 + npre + 1:]
    j = pl.program_id(0)
    s = lax.axis_index('stage')
    PR = PC = 128
    slot = lax.rem(j, 2)

    def out_copy(sl, jj):
        return pltpu.make_async_copy(zs.at[sl], rows_at(z_hbm, jj * BV, BV), sem.at[sl])

    @pl.when(j == 0)
    def _():
        m_s[...] = jnp.full_like(m_s, -jnp.inf)
        s_s[...] = jnp.zeros_like(s_s)
        t_s[...] = jnp.zeros_like(t_s)
        zs[...] = jnp.zeros_like(zs)

    @pl.when(j >= 2)
    def _():
        out_copy(slot, j).wait()

    io = lax.broadcasted_iota(jnp.int32, (SUB, PC), 0)

    def stats(sl, h, jj, dead=None):
        blk = pl.multiple_of((s ^ (k0 + h)) * TB, TB)
        for cc in range(TB // PC):
            c = cols(h * (TB // PC) + cc, PC)
            mo, so, to = m_s[:, c], s_s[:, c], t_s[:, c]
            lab = row(lab_ref, 0, pl.ds(blk + cc * PC, PC)) - (s * V + jj * BV)
            for rr in range(BV // PR):
                gs = [zs[sl, cols(rr * (PR // SUB) + g, SUB), c] for g in range(PR // SUB)]
                mn = jnp.maximum(mo, tree(jnp.maximum, gs))
                so = so * jnp.exp(mo - mn) + tree(jnp.add, [jnp.exp(g - mn) for g in gs])
                mo = mn
                to = to + tree(jnp.add, [jnp.where(io == lab - (rr * PR + g * SUB), v, 0.0) for g, v in enumerate(gs)])
            if dead is not None:
                mo, so, to = jnp.where(dead, -jnp.inf, mo), jnp.where(dead, 0.0, so), jnp.where(dead, 0.0, to)
            m_s[:, c], s_s[:, c], t_s[:, c] = mo, so, to

    for h, xr in enumerate((xa_ref, xb_ref)):
        stats(1 - slot, h, j - 1, j == 0)
        zs[slot, :, cols(h)] = cdot(w_ref[...], xr[...], 1, 1)
    out_copy(slot, j).start()

    @pl.when(j == NT - 1)
    def _():
        for h in range(2):
            stats(slot, h, j)
        m8 = m_s[...]
        m = jnp.max(m8, axis=0, keepdims=True)
        c = cols(npre, PAIR)
        st_ref[...] = jnp.zeros_like(st_ref)
        for i, v in enumerate((m, jnp.sum(s_s[...] * jnp.exp(m8 - m), axis=0, keepdims=True), jnp.sum(t_s[...], axis=0, keepdims=True))):
            st_ref[i:i + 1, c] = v
        if npre:
            st_ref[:, :PAIR] = refs[4][...]
        for sl in range(2):
            out_copy(sl, j).wait()


def z_call(xa, xb, lab, w, pre, dep, k0):
    pre = [] if pre is None else [pre]
    w_st = (1 + len(pre)) * PAIR
    return pl.pallas_call(
        functools.partial(z_body, k0, len(pre)),
        grid=(NT,),
        in_specs=[VM, VM, VM, pl.BlockSpec((BV, D), lambda j: (j, 0))] + [VM] * len(pre) + [ANY],
        out_specs=[ANY, VM],
        out_shape=[jax.ShapeDtypeStruct((V, PAIR), F32), jax.ShapeDtypeStruct((SUB, w_st), F32)],
        scratch_shapes=[pltpu.VMEM((SUB, PAIR), F32)] * 3 + [pltpu.VMEM((2, BV, PAIR), F32), pltpu.SemaphoreType.DMA((2,))],
        compiler_params=params(),
        cost_estimate=HEAD_COST,
    )(xa, xb, lab, w, *pre, dep)


def join_body(*refs):
    own, oth = refs[:4], refs[4:8]
    lo_ref, mo_ref, lx_ref, mx_ref, po_ref, px_ref, loss_ref = refs[8:]
    s = lax.axis_index('stage')
    total = None
    for sts, l_ref, k_ref, p_ref in ((own, lo_ref, mo_ref, po_ref), (oth, lx_ref, mx_ref, px_ref)):
        n = jnp.maximum(jnp.sum(k_ref[...].astype(F32), axis=1, keepdims=True), 1.0)
        parts = []
        for k in range(4):
            blk = pl.ds(pl.multiple_of((s ^ k) * TB, TB), TB)
            ms, ss, ts = [[row(st, i, cols(k ^ q)) for q, st in enumerate(sts)] for i in range(3)]
            m = tree(jnp.maximum, ms)
            z = tree(jnp.add, [v * jnp.exp(u - m) for u, v in zip(ms, ss)])
            t = tree(jnp.add, ts)
            mk = row(k_ref, 0, blk).astype(F32)
            sc = mk / n
            lab = (row(l_ref, 0, blk) - s * V).astype(F32)
            for i, v in enumerate((m, sc / z, sc, lab, sc, sc, sc, sc)):
                p_ref[i:i + 1, cols(k)] = v
            parts.append(jnp.sum(mk * (jnp.log(z) + m - t), axis=1, keepdims=True))
        rep = tree(jnp.add, parts) / n
        total = rep if total is None else total + rep
    loss_ref[...] = jnp.broadcast_to(total * 0.5, loss_ref.shape)


def join_call(own, oth, ints):
    return pl.pallas_call(
        join_body,
        in_specs=[VM] * 12,
        out_specs=[VM] * 3,
        out_shape=[jax.ShapeDtypeStruct((SUB, ALL), F32)] * 2 + [jax.ShapeDtypeStruct((1, 128), F32)],
        compiler_params=params(16),
        cost_estimate=cost(2e9, 2**20),
        name="join",
    )(*own, *oth, *ints)


def gfun(z, p, base):
    m, a, sc, lab = (row(p, i) for i in range(4))
    return jnp.exp(z - m) * a - jnp.where(base == lab, sc, 0.0)


def emb_body(ks, ids_ref, idv_ref, e_hbm, dep_ref, oa_ref, ob_ref, buf, cnt, sem):
    g = pl.program_id(0)
    s = lax.axis_index('stage')
    ng = TB // EG

    def issue(gg, slot):
        n = jnp.int32(0)
        for h, k in enumerate(ks):
            first = (s ^ k) * TB + gg * EG

            def one(t, c):
                i = ids_ref[first + t] - s * V
                ok = (i >= 0) & (i < V)

                @pl.when(ok)
                def _():
                    pltpu.make_async_copy(
                        rows_at(e_hbm, (i // SUB) * SUB, SUB),
                        rows_at(buf.at[slot, h], t * SUB, SUB),
                        sem.at[slot],
                    ).start()

                return c + ok.astype(jnp.int32)

            n = lax.fori_loop(0, EG, one, n, unroll=4)
        cnt[slot] = n

    @pl.when(g == 0)
    def _():
        buf[...] = jnp.zeros_like(buf)
        issue(0, 0)

    slot = lax.rem(g, 2)

    @pl.when(g + 1 < ng)
    def _():
        issue(g + 1, 1 - slot)

    def wait(t, c):
        pltpu.make_async_copy(rows_at(e_hbm, 0, SUB), rows_at(buf.at[slot, 0], 0, SUB), sem.at[slot]).wait()
        return c

    lax.fori_loop(0, cnt[slot], wait, 0)

    lane = lax.broadcasted_iota(jnp.int32, (1, LANES), 1)
    for h, (k, o) in enumerate(zip(ks, (oa_ref, ob_ref))):
        at = pl.multiple_of((s ^ k) * TB + (g // 2) * LANES, LANES)
        i = row(idv_ref, 0, pl.ds(at, LANES)) - s * V
        i = jnp.where((i >= 0) & (i < V), (lane % EG) * SUB + i % SUB, -1)
        i = jnp.where(slot == 0, i[:, :EG], i[:, EG:])
        oh = (lax.broadcasted_iota(jnp.int32, (EG * SUB, EG), 0) == i).astype(F32).astype(BF)
        o[...] = cdot(oh, buf[slot, h], 0, 0).astype(BF)


def emb_call(ids, e, dep, ks):
    gs = pltpu.PrefetchScalarGridSpec(
        num_scalar_prefetch=1,
        grid=(TB // EG,),
        in_specs=[VM, ANY, ANY],
        out_specs=[pl.BlockSpec((EG, D), lambda g, *_: (g, 0))] * 2,
        scratch_shapes=[pltpu.VMEM((2, 2, EG * SUB, D), BF), pltpu.SMEM((2,), jnp.int32), pltpu.SemaphoreType.DMA((2,))],
    )
    return pl.pallas_call(
        functools.partial(emb_body, ks),
        grid_spec=gs,
        out_shape=[jax.ShapeDtypeStruct((TB, D), BF)] * 2,
        compiler_params=params(),
        cost_estimate=cost(1e10, 2**24),
    )(ids, ids.reshape(1, -1), e, dep)


def d_body(nr, c0, sizes, off_ref, *refs):
    ns = len(sizes)
    xs_hbm, (po_ref, px_ref, z1_ref, z2_ref, w_ref) = refs[:8], refs[8:13]
    xs, gt, ob, xsem, osem = refs[-5:]
    g_hbm, *snd = refs[-6 - ns:-5]
    j = pl.program_id(0)
    nt = nr + sum(sizes)
    r = off_ref[1]
    own = pl.multiple_of(r * ALL, ALL)
    oth = pl.multiple_of((1 - r) * ALL, ALL)
    tile = jnp.where(j < nr, 2 * A + j, off_ref[0] + c0 + j - nr)
    slot = lax.rem(j, 2)

    def out_copy(dst, at, sl, which):
        return pltpu.make_async_copy(ob.at[sl], rows_at(dst, at, BV), osem.at[sl, which])

    @pl.when(j == 0)
    def _():
        copy_all([pltpu.make_async_copy(x, rows_at(xs, (own if i < 4 else oth) + (i % 4) * TB, TB), xsem.at[i])
                  for i, x in enumerate(xs_hbm)])

    @pl.when(j >= 2)
    def _():
        out_copy(g_hbm, 0, slot, 0).wait()

    @pl.when(j >= 2 + nr)
    def _():
        out_copy(snd[0], 0, slot, 1).wait()

    base = (lax.broadcasted_iota(jnp.int32, (BV, 1), 0) + tile * BV).astype(F32)
    for tb in range(4):
        zr = (z1_ref, z2_ref)[tb // 2]
        gt[:, pl.ds(own + tb * TB, TB)] = gfun(zr[:, cols(tb % 2)], po_ref[:, cols(tb)], base).astype(BF)
    for tb in range(4):
        zt = cdot(w_ref[...], xs[pl.ds(oth + tb * TB, TB), :], 1, 1)
        gt[:, pl.ds(oth + tb * TB, TB)] = gfun(zt, px_ref[:, cols(tb)], base).astype(BF)
    for n in range(D // CB):
        ob[slot, :, cols(n, CB)] = (cdot(gt[...], xs[:, cols(n, CB)], 1, 0) * 0.5).astype(BF)

    out_copy(g_hbm, tile * BV, slot, 0).start()
    lo = nr
    for i, sz in enumerate(sizes):
        @pl.when((j >= lo) & (j < lo + sz))
        def _(i=i, lo=lo):
            out_copy(snd[i], (j - lo) * BV, slot, 1).start()

        lo += sz

    @pl.when(j == nt - 1)
    def _():
        for jj in range(max(nt - 2, 0), nt):
            for which, dst in enumerate((g_hbm, snd[0])[:1 + (jj >= nr)]):
                out_copy(dst, 0, jj % 2, which).wait()


def d_call(off, xs, po, px, z1, z2, w, gin, dep, nr, c0, sizes):
    nt = nr + sum(sizes)
    tile = lambda j, o: (jnp.where(j < nr, 2 * A + j, o[0] + c0 + j - nr), 0)
    ins = [off, *xs, po, px, z1, z2, w]
    specs = [ANY] * 8 + [VM, VM] + [pl.BlockSpec((BV, PAIR), tile)] * 2 + [pl.BlockSpec((BV, D), tile)]
    alias = {}
    if gin is not None:
        alias = {len(ins): 0}
        ins.append(gin)
        specs.append(ANY)
    ins.append(dep)
    specs.append(ANY)
    gs = pltpu.PrefetchScalarGridSpec(
        num_scalar_prefetch=1,
        grid=(nt,),
        in_specs=specs,
        out_specs=[ANY] * (1 + len(sizes)),
        scratch_shapes=[
            pltpu.VMEM((2 * ALL, D), BF),
            pltpu.VMEM((BV, 2 * ALL), BF),
            pltpu.VMEM((2, BV, D), BF),
            pltpu.SemaphoreType.DMA((8,)),
            pltpu.SemaphoreType.DMA((2, 2)),
        ],
    )
    return pl.pallas_call(
        functools.partial(d_body, nr, c0, sizes),
        grid_spec=gs,
        out_shape=[jax.ShapeDtypeStruct((V, D), BF)] + [jax.ShapeDtypeStruct((s * BV, D), BF) for s in sizes],
        input_output_aliases=alias,
        compiler_params=params(),
        cost_estimate=cost(nt * 6 * BV * ALL * D, nt * 12e6 + 21e6),
    )(*ins)


def dx_body(half, p_ref, za0, zb0, zan, zbn, w0, wn, w1, w2, w3, w4, dep_ref, oa_ref, ob_ref, acc, g0, g1, sem):
    j = pl.program_id(0)

    def mkg(dst, za, zb, tile):
        base = (lax.broadcasted_iota(jnp.int32, (BV, 1), 0) + tile * BV).astype(F32)
        for k in range(BV // LANES):
            c = cols(k, LANES)
            for q, zr in enumerate((za, zb)):
                dst[cols(q), c] = gfun(zr[c, :], p_ref[:, cols(half + 2 * q)], base[c]).astype(BF).T

    @pl.when(j == 0)
    def _():
        mkg(g0, za0, zb0, 0)
        acc[...] = jnp.zeros_like(acc)
        acc[:, :CB] = cdot(g0[...], w0[...], 1, 0)

    def step(cur, nxt):
        mkg(nxt, zan, zbn, j + 1)
        for i, w in enumerate((w1, w2, w3, w4)):
            acc[:, cols(i + 1, CB)] += cdot(cur[...], w[...], 1, 0)
        acc[:, :CB] += jnp.where(j == NT - 1, 0.0, cdot(nxt[...], wn[...], 1, 0))

    @pl.when(lax.rem(j, 2) == 0)
    def _():
        step(g0, g1)

    @pl.when(lax.rem(j, 2) == 1)
    def _():
        step(g1, g0)

    @pl.when(j == NT - 1)
    def _():
        copy_all([pltpu.make_async_copy(acc.at[cols(i)], o, sem.at[i]) for i, o in enumerate((oa_ref, ob_ref))])


def dx_call(p, z1, z2, w, dep, half):
    zs = lambda im, **k: pl.BlockSpec((BV, TB), im, **k)
    first = zs(lambda j: (0, half), pipeline_mode=pl.Buffered(1))
    nj = lambda j: jnp.minimum(j + 1, NT - 1)
    nxt = zs(lambda j: (nj(j), half))
    ws = [pl.BlockSpec((BV, CB), lambda j: (0, 0), pipeline_mode=pl.Buffered(1)), pl.BlockSpec((BV, CB), lambda j: (nj(j), 0))]
    ws += [pl.BlockSpec((BV, CB), lambda j, q=q: (j, q)) for q in range(1, D // CB)]
    return pl.pallas_call(
        functools.partial(dx_body, half),
        grid=(NT,),
        in_specs=[VM, first, first, nxt, nxt] + ws + [ANY],
        out_specs=[ANY, ANY],
        out_shape=[jax.ShapeDtypeStruct((TB, D), F32)] * 2,
        scratch_shapes=[pltpu.VMEM((PAIR, D), F32)] + [pltpu.VMEM((PAIR, BV), BF)] * 2 + [
            pltpu.SemaphoreType.DMA((2,))],
        compiler_params=params(),
        cost_estimate=HEAD_COST,
    )(p, z1, z2, z1, z2, *([w] * 6), dep)


def mlp_body(nsrc, split, fb, mb, off_ref, a_ref, w1_ref, w2_ref, *refs):
    src = refs[:nsrc]
    o_ref, g_ref, acc, h_s = refs[nsrc + 2:]
    j = pl.program_id(0)
    rows = PAIR
    n = FF // fb
    nb = rows // mb
    g_ref[...] = src[0][...] if nsrc == 1 else jnp.where(j < split, src[0][...], src[1][...])

    def d1(b):
        r = cols(b, mb)
        h_s[r, :] = jax.nn.gelu(cdot(a_ref[r, :], w1_ref[0], 1, 0)).astype(BF)

    def d2(b):
        r = cols(b, mb)
        for i in range(D // CB):
            c = cols(i, CB)
            acc[r, c] = jnp.where(j == 0, a_ref[r, c].astype(F32), acc[r, c]) + cdot(h_s[r, :], w2_ref[0, :, c], 1, 0)

    d1(0)
    for b in range(1, nb):
        d1(b)
        d2(b - 1)
    d2(nb - 1)

    @pl.when(j == n - 1)
    def _():
        o_ref[...] = acc[...].astype(BF)


def mlp_call(off, a, w1, w2, srcs, gin, dep, row_blk, c0, oin=None, fb=512, mb=256, cb=128):
    n = FF // fb
    rows = PAIR
    nblk = [s.shape[0] // cb for s in srcs]
    tot = sum(nblk)
    split = nblk[0]
    sspecs = [pl.BlockSpec((cb, D), lambda j, o: (jnp.minimum(j, nblk[0] - 1), 0))]
    if len(srcs) > 1:
        sspecs.append(pl.BlockSpec((cb, D), lambda j, o: (jnp.clip(j - split, 0, nblk[1] - 1), 0)))
    t = BV // cb
    gs = pltpu.PrefetchScalarGridSpec(
        num_scalar_prefetch=1,
        grid=(n,),
        in_specs=[pl.BlockSpec((rows, D), lambda j, o: (row_blk, 0), pipeline_mode=pl.Buffered(1)),
                  pl.BlockSpec((1, D, fb), lambda j, o: (0, 0, j)),
                  pl.BlockSpec((1, fb, D), lambda j, o: (0, j, 0))] + sspecs + [ANY, ANY],
        out_specs=[pl.BlockSpec((rows, D), lambda j, o: (row_blk, 0), pipeline_mode=pl.Buffered(1)),
                   pl.BlockSpec((cb, D), lambda j, o: ((A - o[0] + c0) * t + jnp.minimum(j, tot - 1), 0))],
        scratch_shapes=[pltpu.VMEM((rows, D), F32), pltpu.VMEM((rows, fb), BF)],
    )
    k = 4 + len(srcs)
    alias = {k: 1}
    if oin is not None:
        alias[k + 1] = 0
        dep = oin
    return pl.pallas_call(
        functools.partial(mlp_body, len(srcs), split, fb, mb),
        grid_spec=gs,
        out_shape=[jax.ShapeDtypeStruct((ALL, D), BF), jax.ShapeDtypeStruct((V, D), BF)],
        input_output_aliases=alias,
        compiler_params=params(),
        cost_estimate=cost(4 * rows * FF * D, 110e6),
    )(off, a, w1, w2, *srcs, gin, dep)


def put_body(off_ref, s_ref, gin_ref, g_ref):
    g_ref[...] = s_ref[...]


def put_call(off, src, gin, c0, cb=256):
    n = src.shape[0] // cb
    gs = pltpu.PrefetchScalarGridSpec(
        num_scalar_prefetch=1,
        grid=(n,),
        in_specs=[pl.BlockSpec((cb, D), lambda j, o: (j, 0)), ANY],
        out_specs=pl.BlockSpec((cb, D), lambda j, o: ((A - o[0] + c0) * (BV // cb) + j, 0)),
    )
    return pl.pallas_call(
        put_body,
        grid_spec=gs,
        out_shape=jax.ShapeDtypeStruct((V, D), BF),
        input_output_aliases={2: 0},
        compiler_params=params(),
        cost_estimate=cost(1e9, 2 * src.size * 2),
        name="put",
    )(off, src, gin)


def solution(mesh):
    tok_spec = P(('pod', 'data', 'stage'), None)
    rep_spec = P(('pod', 'data'))
    vocab_spec = P('stage', None)
    layer_spec = P('stage', None, None)

    def px(a, q):
        return lax.ppermute(a, 'stage', [(i, i ^ q) for i in range(4)])

    def py(a, q=0):
        if q == 0:
            return lax.ppermute(a, 'data', [(0, 1), (1, 0)])
        return lax.ppermute(a, ('data', 'stage'), [(i, i ^ 4 ^ q) for i in range(8)])

    def local_step(x, w_head, labels, loss_mask, w_embed, tok_ids, act_in, w_up, w_down):
        r = lax.axis_index('data')
        off = jnp.stack([r * A, r]).astype(jnp.int32)

        x1 = px(x, 1)
        x2 = px(x, 2)
        xo0 = py(x)
        x3 = px(x2, 1)
        xo2 = px(xo0, 2)
        xo1 = px(xo0, 1)
        xo3 = px(xo2, 1)
        lab = labels.reshape(1, -1)
        msk = loss_mask.reshape(1, -1)
        labx = py(lab)
        mskx = py(msk)

        z1, st1 = z_call(x, x1, lab, w_head, None, x, 0)
        e1, e3 = emb_call(tok_ids, w_embed, st1, (1, 3))
        z2, st = z_call(x2, x3, lab, w_head, st1, e1, 2)
        own = [px(st, q) if q else st for q in range(4)]
        oth = [py(st, q) for q in range(4)]
        re1 = px(e1, 1)
        re3 = px(e3, 1)
        e0, e2 = emb_call(tok_ids, w_embed, st, (0, 2))
        po, pxx, loss = join_call(own, oth, [lab, msk, labx, mskx])
        re2 = px(e2 + re3, 2)

        xs = [x, x1, x2, x3, xo0, xo1, xo2, xo3]
        g, rcv, at = None, [], []
        for i, (nr, sizes) in enumerate(CALLS):
            c0 = sum(sum(q) for _, q in CALLS[:i])
            g, *snd = d_call(off, xs, po, pxx, z1, z2, w_head, g, e0, nr, c0, sizes)
            for a, q in zip(snd, sizes):
                rcv.append(py(a))
                at.append(c0)
                c0 += q

        dx1, dx3 = dx_call(po, z1, z2, w_head, g, 1)
        rd1 = px(dx1, 1)
        rd3 = px(dx3, 1)
        dx0, dx2 = dx_call(po, z1, z2, w_head, dx1, 0)
        rd2 = px(dx2 + rd3, 2)

        m, g = mlp_call(off, act_in, w_up, w_down, rcv[:2], g, dx0, 0, at[0])
        m, g = mlp_call(off, act_in, w_up, w_down, rcv[2:3], g, m, 1, at[2], oin=m)
        g = put_call(off, rcv[3], g, at[3])

        grad_x = (dx0 + rd1) + rd2
        emb = (e0 + re1) + re2
        return loss[0, :1], grad_x, g, emb, m

    return jax.shard_map(
        local_step,
        mesh=mesh,
        in_specs=(tok_spec, vocab_spec, rep_spec, rep_spec, vocab_spec, rep_spec, tok_spec, layer_spec, layer_spec),
        out_specs=(P('pod'), tok_spec, P(('pod', 'stage'), None), tok_spec, tok_spec),
        check_vma=False,
    )
```

time: 3570 us -> 1340 us (0.38)
  waiting for transfers between devices: 2550 us -> 308 us
  Pallas kernels: 0 us -> 969 us
  matrix products: 714 us -> 0 us
  other arithmetic: 160 us -> 26.2 us
  local copies, waits for them, and re-layouts: 98.9 us -> 1.29 us
    psum x1 -> x0, waiting for transfers between devices: 2310 us -> none  [local_step(): grad_head = (lax.psum(dw_part, 'data') / n_data).astype(jnp.bfloat16)]
    pallas_call x0 -> x13, Pallas kernels: none -> 969 us  [the longest x3 288 us: d_call(): pl.pallas_call(functools.partial(d_body, nr, c0, sizes), grid_spec=gs, ou...]
    dot_general x5 -> x0, matrix products: 714 us -> none  [the longest x1 158 us: local_step(): jnp.einsum('tv,td->vd', grad_logits, x_full, preferred_element_type=jnp.f...]
    ppermute x0 -> x26, waiting for transfers between devices: none -> 308 us  [the longest x8 305 us: py(): return lax.ppermute(a, 'data', [(0, 1), (1, 0)])]
    reduce_scatter x2 -> x0, waiting for transfers between devices: 168 us -> none  [the longest x1 147 us: local_step(): grad_x = lax.psum_scatter(dx_part, 'stage', scatter_dimension=0, tiled=True)]
    convert_element_type x2 -> x0, other arithmetic: 113 us -> none  [the longest x1 62.1 us: local_step(): grad_head = (lax.psum(dw_part, 'data') / n_data).astype(jnp.bfloat16)]
    gather x1 -> x0, local copies, waits for them, and re-layouts: 98.3 us -> none  [local_step(): rows_emb = jnp.take(w_embed, jnp.clip(local_ids, 0, slice_rows - 1), axis=0)]
    all_gather x1 -> x0, waiting for transfers between devices: 71.6 us -> none  [local_step(): x_full = lax.all_gather(x_rows, 'stage', axis=0, tiled=True)]
  transfers between devices with their start and end apart: 4 -> 26, of which waited for: 4 -> 6; matrix products, arithmetic and copies ran while one was open for 16% -> 2% of each run, Pallas kernels for 0% -> 72%
where the time goes in v1:
time: 1340 us; the launch traced here: 1330 us
  Pallas kernels  969 us (72%)
  waiting for transfers between devices  308 us (23%)
  other arithmetic  26.2 us (2%)
  starting transfers between devices  21.9 us (2%)
    ppermute x8, waiting for transfers between devices, py(): return lax.ppermute(a, 'data', [(0, 1), (1, 0)])  305 us
    pallas_call x3, Pallas kernels, d_call(): pl.pallas_call(functools.partial(d_body, nr, c0, sizes), grid_spec=gs, ou...  288 us
    pallas_call x2, Pallas kernels, mlp_call(): pl.pallas_call(functools.partial(mlp_body, len(srcs), split, fb, mb), gri...  256 us
    pallas_call x2, Pallas kernels, z_call(): pl.pallas_call(functools.partial(z_body, k0, len(pre)), grid=(NT,), in_sp...  185 us
    pallas_call x2, Pallas kernels, dx_call(): pl.pallas_call(functools.partial(dx_body, half), grid=(NT,), in_specs=[VM...  180 us
    pallas_call x2, Pallas kernels, emb_call(): pl.pallas_call(functools.partial(emb_body, ks), grid_spec=gs, out_shape=[...  50.7 us
  transfers between devices with their start and end apart: 26, of which 6 were waited for; matrix products, arithmetic and copies ran while one was open for 2% of the time, Pallas kernels for 72%

profile of v1, /device:TPU:0, one launch (start us, length us, event | category | flops | bytes accessed | tf_op | source)
XLA Modules:
  0.0 1327.9 jit_solution(12307772074491177618)
XLA Ops:
  0.6 3.4 collective-permute-start.12
  4.0 1.5 collective-permute-start
  5.5 55.7 %collective-permute-done.12.refs_4_ = bf16[512,2560]{1,0:T(8,128)(2,1)} collective-permute-done((bf16[512,2560]{1,0:T(8,128)(2,1)}, bf16[512,2560]{1,0:T(8,128)(2,1)}, u32[]{:S(2)}, u32[]{:S(2)}) %collective-permute-start.12) | collective-permute-done | bytes 2621472 | tf_op jit(solution)/shard_map/ppermute | solution.py:506
  61.2 1.7 collective-permute-start.14
  62.9 92.4 %shard_map.128 = (f32[12800,1024]{1,0:T(8,128)}, f32[8,1024]{1,0:T(8,128)}) custom-call(bf16[512,2560]{1,0:T(8,128)(2,1)} %refs_0_.7, bf16[512,2560]{1,0:T(8,128)(2,1)} %collective-permute-done.2.refs_1_, s32[1,2048]{1,0:T(1,128)} %bitcast.7, bf16[12800,2560]{1,0:T(8,128)(2,1)} %w4.3, bf16[512,2560]{1,0:T(8,128)(2,1)} %refs_0_.7), custom_call_target="tpu_custom_call" | custom-call | flops 67108864000 | bytes 117964800 | tf_op jit(solution)/shard_map/pallas_call | solution.py:137
  155.3 25.2 %shard_map.129 = (bf16[512,2560]{1,0:T(8,128)(2,1)}, bf16[512,2560]{1,0:T(8,128)(2,1)}) custom-call(s32[2048]{0:T(1024)} %ids_ref.3, s32[1,2048]{1,0:T(1,128)} %bitcast.15, bf16[12800,2560]{1,0:T(8,128)(2,1)} %e_hbm.3, f32[8,1024]{1,0:T(8,128)} %get-tuple-element.31.dep_ref.refs_4_), custom_call_target="tpu_custom_call" | custom-call | flops 10000000000 | bytes 16777216 | tf_op jit(solution)/shard_map/pallas_call | solution.py:253
  181.5 92.4 %shard_map.130 = (f32[12800,1024]{1,0:T(8,128)}, f32[8,2048]{1,0:T(8,128)}) custom-call(bf16[512,2560]{1,0:T(8,128)(2,1)} %collective-permute-done.refs_0_.refs_2_, bf16[512,2560]{1,0:T(8,128)(2,1)} %collective-permute-done.1.refs_1_.refs_3_, s32[1,2048]{1,0:T(1,128)} %bitcast.8, bf16[12800,2560]{1,0:T(8,128)(2,1)} %w4.3, ...), custom_call_target="tpu_custom_call" | custom-call | flops 67108864000 | bytes 117964800 | tf_op jit(solution)/shard_map/pallas_call | solution.py:137
  276.2 3.3 collective-permute-done.10.refs_10_
  280.7 2.5 collective-permute-done.11.refs_11_
  286.5 2.2 collective-permute-done.8.refs_6_
  291.1 25.5 %shard_map.131 = (bf16[512,2560]{1,0:T(8,128)(2,1)}, bf16[512,2560]{1,0:T(8,128)(2,1)}) custom-call(s32[2048]{0:T(1024)} %ids_ref.3, s32[1,2048]{1,0:T(1,128)} %bitcast.16, bf16[12800,2560]{1,0:T(8,128)(2,1)} %e_hbm.3, f32[8,2048]{1,0:T(8,128)} %get-tuple-element.33.refs_0_.dep_ref), custom_call_target="tpu_custom_call" | custom-call | flops 10000000000 | bytes 16777216 | tf_op jit(solution)/shard_map/pallas_call | solution.py:253
  316.7 4.7 add.22
  324.7 30.8 %shard_map.132 = (bf16[12800,2560]{1,0:T(8,128)(2,1)}, bf16[512,2560]{1,0:T(8,128)(2,1)}) custom-call(s32[2]{0:T(128)} %pad_add_fusion.off_ref, bf16[512,2560]{1,0:T(8,128)(2,1)} %refs_0_.7, bf16[512,2560]{1,0:T(8,128)(2,1)} %collective-permute-done.2.refs_1_, bf16[512,2560]{1,0:T(8,128)(2,1)} %collective-permute-done.refs_0_.refs_2_, ...), custom_call_target="tpu_custom_call" | custom-call | flops 16106127360 | bytes 33000000 | tf_op jit(solution)/shard_map/pallas_call | solution.py:342
  356.5 67.2 %shard_map.133 = (bf16[12800,2560]{1,0:T(8,128)(2,1)}, bf16[1536,2560]{1,0:T(8,128)(2,1)}) custom-call(s32[2]{0:T(128)} %pad_add_fusion.off_ref, bf16[512,2560]{1,0:T(8,128)(2,1)} %refs_0_.7, bf16[512,2560]{1,0:T(8,128)(2,1)} %collective-permute-done.2.refs_1_, ...), custom_call_target="tpu_custom_call", output_to_operand_aliasing={{0}: (14, {})} | custom-call | flops 48318382080 | bytes 57000000 | tf_op jit(solution)/shard_map/pallas_call | solution.py:342
  424.7 190.3 %shard_map.134 = (bf16[12800,2560]{1,0:T(8,128)(2,1)}, bf16[2048,2560]{1,0:T(8,128)(2,1)}, bf16[1536,2560]{1,0:T(8,128)(2,1)}) custom-call(s32[2]{0:T(128)} %pad_add_fusion.off_ref, bf16[512,2560]{1,0:T(8,128)(2,1)} %refs_0_.7, bf16[512,2560]{1,0:T(8,128)(2,1)} %collective-permute-done.2.refs_1_, ...), custom_call_target="tpu_custom_call", output_to_operand_aliasing={{0}: (14, {})} | custom-call | flops 161061273600 | bytes 141000000 | tf_op jit(solution)/shard_map/pallas_call | solution.py:342
  615.0 90.5 %shard_map.135 = (f32[512,2560]{1,0:T(8,128)}, f32[512,2560]{1,0:T(8,128)}) custom-call(f32[8,2048]{1,0:T(8,128)} %copy-done, f32[12800,1024]{1,0:T(8,128)} %get-tuple-element.36.refs_10_.za0.zan, f32[12800,1024]{1,0:T(8,128)} %get-tuple-element.37.refs_11_.zb0.zbn, f32[12800,1024]{1,0:T(8,128)} %get-tuple-element.36.refs_10_.za0.zan, ...), custom_call_target="tpu_custom_call" | custom-call | flops 67108864000 | bytes 117964800 | tf_op jit(solution)/shard_map/pallas_call | solution.py:394
  705.5 89.9 %shard_map.136 = (f32[512,2560]{1,0:T(8,128)}, f32[512,2560]{1,0:T(8,128)}) custom-call(f32[8,2048]{1,0:T(8,128)} %copy-done, f32[12800,1024]{1,0:T(8,128)} %get-tuple-element.36.refs_10_.za0.zan, f32[12800,1024]{1,0:T(8,128)} %get-tuple-element.37.refs_11_.zb0.zbn, f32[12800,1024]{1,0:T(8,128)} %get-tuple-element.36.refs_10_.za0.zan, ...), custom_call_target="tpu_custom_call" | custom-call | flops 67108864000 | bytes 117964800 | tf_op jit(solution)/shard_map/pallas_call | solution.py:394
  797.0 5.7 add_add_fusion.1
  803.6 5.7 add.19
  810.5 128.9 %shard_map.137 = (bf16[2048,2560]{1,0:T(8,128)(2,1)}, bf16[12800,2560]{1,0:T(8,128)(2,1)}) custom-call(s32[2]{0:T(128)} %pad_add_fusion.off_ref, bf16[2048,2560]{1,0:T(8,128)(2,1)} %a_ref.3, bf16[1,2560,10240]{2,1,0:T(8,128)(2,1)} %w1_ref.3, bf16[1,10240,2560]{2,1,0:T(8,128)(2,1)} %w2_ref.3, ...), custom_call_target="tpu_custom_call", output_to_operand_aliasing={{1}: (6, {})} | custom-call | flops 107374182400 | bytes 110000000 | tf_op jit(solution)/shard_map/pallas_call | solution.py:462
  939.4 9.6 add_add_fusion
  949.0 243.1 %collective-permute-done.20.refs_0_ = bf16[2048,2560]{1,0:T(8,128)(2,1)} collective-permute-done((bf16[2048,2560]{1,0:T(8,128)(2,1)}, bf16[2048,2560]{1,0:T(8,128)(2,1)}, u32[]{:S(2)}, u32[]{:S(2)}) %collective-permute-start.20) | collective-permute-done | bytes 10485792 | tf_op jit(solution)/shard_map/ppermute | solution.py:506
  1192.1 127.2 %shard_map.138 = (bf16[2048,2560]{1,0:T(8,128)(2,1)}, bf16[12800,2560]{1,0:T(8,128)(2,1)}) custom-call(s32[2]{0:T(128)} %pad_add_fusion.off_ref, bf16[2048,2560]{1,0:T(8,128)(2,1)} %a_ref.3, bf16[1,2560,10240]{2,1,0:T(8,128)(2,1)} %w1_ref.3, bf16[1,10240,2560]{2,1,0:T(8,128)(2,1)} %w2_ref.3, ...), custom_call_target="tpu_custom_call", output_to_operand_aliasing={{1}: (5, {}), {0}: (6, {})} | custom-call | flops 107374182400 | bytes 110000000 | tf_op jit(solution)/shard_map/pallas_call | solution.py:462
  1319.3 8.4 put.1
  (61 shorter events, 19.2 us)
Async XLA Ops:
  0.6 60.5 %collective-permute-start.12 = (bf16[512,2560]{1,0:T(8,128)(2,1)}, bf16[512,2560]{1,0:T(8,128)(2,1)}, u32[]{:S(2)}, u32[]{:S(2)}) collective-permute-start(bf16[512,2560]{1,0:T(8,128)(2,1)} %refs_0_.7), channel_id=1, source_target_pairs={{0,4},{4,0},{1,5},{5,1},{2,6},{6,2},{3,7},{7,3}} | collective-permute-start | bytes 7864328 | tf_op jit(solution)/shard_map/ppermute | solution.py:506
  4.0 58.9 %collective-permute-start = (bf16[512,2560]{1,0:T(8,128)(2,1)}, bf16[512,2560]{1,0:T(8,128)(2,1)}, u32[]{:S(2)}, u32[]{:S(2)}) collective-permute-start(bf16[512,2560]{1,0:T(8,128)(2,1)} %refs_0_.7), channel_id=1, source_target_pairs={{0,2},{1,3},{2,0},{3,1},{4,6},{5,7},{6,4},{7,5}} | collective-permute-start | bytes 7864328 | tf_op jit(solution)/shard_map/ppermute | solution.py:502
  5.5 57.4 %collective-permute-start.2 = (bf16[512,2560]{1,0:T(8,128)(2,1)}, bf16[512,2560]{1,0:T(8,128)(2,1)}, u32[]{:S(2)}, u32[]{:S(2)}) collective-permute-start(bf16[512,2560]{1,0:T(8,128)(2,1)} %refs_0_.7), channel_id=1, source_target_pairs={{0,1},{1,0},{2,3},{3,2},{4,5},{5,4},{6,7},{7,6}} | collective-permute-start | bytes 7864328 | tf_op jit(solution)/shard_map/ppermute | solution.py:502
  61.2 119.9 %collective-permute-start.14 = (bf16[512,2560]{1,0:T(8,128)(2,1)}, bf16[512,2560]{1,0:T(8,128)(2,1)}, u32[]{:S(2)}, u32[]{:S(2)}) collective-permute-start(bf16[512,2560]{1,0:T(8,128)(2,1)} %collective-permute-done.12.refs_4_), channel_id=1, source_target_pairs={{0,2},{1,3},{2,0},{3,1},{4,6},{5,7},{6,4},{7,5}} | collective-permute-start | bytes 7864328 | tf_op jit(solution)/shard_map/ppermute | solution.py:502
  62.9 118.6 %collective-permute-start.1 = (bf16[512,2560]{1,0:T(8,128)(2,1)}, bf16[512,2560]{1,0:T(8,128)(2,1)}, u32[]{:S(2)}, u32[]{:S(2)}) collective-permute-start(bf16[512,2560]{1,0:T(8,128)(2,1)} %collective-permute-done.refs_0_.refs_2_), channel_id=1, source_target_pairs={{0,1},{1,0},{2,3},{3,2},{4,5},{5,4},{6,7},{7,6}} | collective-permute-start | bytes 7864328 | tf_op jit(solution)/shard_map/ppermute | solution.py:502
  180.5 104.2 %collective-permute-start.24 = (bf16[512,2560]{1,0:T(8,128)(2,1)}, bf16[512,2560]{1,0:T(8,128)(2,1)}, u32[]{:S(2)}, u32[]{:S(2)}) collective-permute-start(bf16[512,2560]{1,0:T(8,128)(2,1)} %get-tuple-element.55), channel_id=1, source_target_pairs={{0,1},{1,0},{2,3},{3,2},{4,5},{5,4},{6,7},{7,6}} | collective-permute-start | bytes 7864328 | tf_op jit(solution)/shard_map/ppermute | solution.py:502
  180.9 143.7 %collective-permute-start.13 = (bf16[512,2560]{1,0:T(8,128)(2,1)}, bf16[512,2560]{1,0:T(8,128)(2,1)}, u32[]{:S(2)}, u32[]{:S(2)}) collective-permute-start(bf16[512,2560]{1,0:T(8,128)(2,1)} %collective-permute-done.12.refs_4_), channel_id=1, source_target_pairs={{0,1},{1,0},{2,3},{3,2},{4,5},{5,4},{6,7},{7,6}} | collective-permute-start | bytes 7864328 | tf_op jit(solution)/shard_map/ppermute | solution.py:502
  181.0 143.6 %collective-permute-start.15 = (bf16[512,2560]{1,0:T(8,128)(2,1)}, bf16[512,2560]{1,0:T(8,128)(2,1)}, u32[]{:S(2)}, u32[]{:S(2)}) collective-permute-start(bf16[512,2560]{1,0:T(8,128)(2,1)} %collective-permute-done.14.refs_6_), channel_id=1, source_target_pairs={{0,1},{1,0},{2,3},{3,2},{4,5},{5,4},{6,7},{7,6}} | collective-permute-start | bytes 7864328 | tf_op jit(solution)/shard_map/ppermute | solution.py:502
  273.9 10.8 collective-permute-start.9
  283.2 5.5 collective-permute-start.8
  284.7 5.3 collective-permute-start.7
  284.7 6.4 collective-permute-start.6
  288.7 32.6 %collective-permute-start.5 = (f32[8,2048]{1,0:T(8,128)}, f32[8,2048]{1,0:T(8,128)S(1)}, u32[]{:S(2)}, u32[]{:S(2)}) collective-permute-start(f32[8,2048]{1,0:T(8,128)} %get-tuple-element.33.refs_0_.dep_ref), channel_id=1, source_target_pairs={{0,3},{1,2},{2,1},{3,0},{4,7},{5,6},{6,5},{7,4}} | collective-permute-start | bytes 196616 | tf_op jit(solution)/shard_map/ppermute | solution.py:502
  290.0 31.9 %collective-permute-start.4 = (f32[8,2048]{1,0:T(8,128)}, f32[8,2048]{1,0:T(8,128)S(1)}, u32[]{:S(2)}, u32[]{:S(2)}) collective-permute-start(f32[8,2048]{1,0:T(8,128)} %get-tuple-element.33.refs_0_.dep_ref), channel_id=1, source_target_pairs={{0,2},{1,3},{2,0},{3,1},{4,6},{5,7},{6,4},{7,5}} | collective-permute-start | bytes 196616 | tf_op jit(solution)/shard_map/ppermute | solution.py:502
  291.1 31.6 %collective-permute-start.3 = (f32[8,2048]{1,0:T(8,128)}, f32[8,2048]{1,0:T(8,128)S(1)}, u32[]{:S(2)}, u32[]{:S(2)}) collective-permute-start(f32[8,2048]{1,0:T(8,128)} %get-tuple-element.33.refs_0_.dep_ref), channel_id=1, source_target_pairs={{0,1},{1,0},{2,3},{3,2},{4,5},{5,4},{6,7},{7,6}} | collective-permute-start | bytes 196616 | tf_op jit(solution)/shard_map/ppermute | solution.py:502
  321.4 474.0 %collective-permute-start.23 = (bf16[512,2560]{1,0:T(8,128)(2,1)}, bf16[512,2560]{1,0:T(8,128)(2,1)}, u32[]{:S(2)}, u32[]{:S(2)}) collective-permute-start(bf16[512,2560]{1,0:T(8,128)(2,1)} %get-tuple-element.32.refs_5_), channel_id=1, source_target_pairs={{0,1},{1,0},{2,3},{3,2},{4,5},{5,4},{6,7},{7,6}} | collective-permute-start | bytes 7864328 | tf_op jit(solution)/shard_map/ppermute | solution.py:502
  321.9 474.0 %collective-permute-start.25 = (bf16[512,2560]{1,0:T(8,128)(2,1)}, bf16[512,2560]{1,0:T(8,128)(2,1)}, u32[]{:S(2)}, u32[]{:S(2)}) collective-permute-start(bf16[512,2560]{1,0:T(8,128)(2,1)} %add.22), channel_id=1, source_target_pairs={{0,2},{1,3},{2,0},{3,1},{4,6},{5,7},{6,4},{7,5}} | collective-permute-start | bytes 7864328 | tf_op jit(solution)/shard_map/ppermute | solution.py:502
  355.4 453.8 %collective-permute-start.21 = (bf16[512,2560]{1,0:T(8,128)(2,1)}, bf16[512,2560]{1,0:T(8,128)(2,1)}, u32[]{:S(2)}, u32[]{:S(2)}) collective-permute-start(bf16[512,2560]{1,0:T(8,128)(2,1)} %get-tuple-element.49), channel_id=1, source_target_pairs={{0,4},{4,0},{1,5},{5,1},{2,6},{6,2},{3,7},{7,3}} | collective-permute-start | bytes 7864328 | tf_op jit(solution)/shard_map/ppermute | solution.py:506
  423.7 386.8 %collective-permute-start.22 = (bf16[1536,2560]{1,0:T(8,128)(2,1)}, bf16[1536,2560]{1,0:T(8,128)(2,1)}, u32[]{:S(2)}, u32[]{:S(2)}) collective-permute-start(bf16[1536,2560]{1,0:T(8,128)(2,1)} %get-tuple-element.50), channel_id=1, source_target_pairs={{0,4},{4,0},{1,5},{5,1},{2,6},{6,2},{3,7},{7,3}} | collective-permute-start | bytes 23592968 | tf_op jit(solution)/shard_map/ppermute | solution.py:506
  705.4 97.2 %collective-permute-start.17 = (f32[512,2560]{1,0:T(8,128)}, f32[512,2560]{1,0:T(8,128)}, u32[]{:S(2)}, u32[]{:S(2)}) collective-permute-start(f32[512,2560]{1,0:T(8,128)} %get-tuple-element.46), channel_id=1, source_target_pairs={{0,1},{1,0},{2,3},{3,2},{4,5},{5,4},{6,7},{7,6}} | collective-permute-start | bytes 15728648 | tf_op jit(solution)/shard_map/ppermute | solution.py:502
  795.4 144.0 %collective-permute-start.16 = (f32[512,2560]{1,0:T(8,128)}, f32[512,2560]{1,0:T(8,128)}, u32[]{:S(2)}, u32[]{:S(2)}) collective-permute-start(f32[512,2560]{1,0:T(8,128)} %get-tuple-element.43.dep_ref), channel_id=1, source_target_pairs={{0,1},{1,0},{2,3},{3,2},{4,5},{5,4},{6,7},{7,6}} | collective-permute-start | bytes 15728648 | tf_op jit(solution)/shard_map/ppermute | solution.py:502
  795.9 523.4 %collective-permute-start.19 = (bf16[1536,2560]{1,0:T(8,128)(2,1)}, bf16[1536,2560]{1,0:T(8,128)(2,1)}, u32[]{:S(2)}, u32[]{:S(2)}) collective-permute-start(bf16[1536,2560]{1,0:T(8,128)(2,1)} %get-tuple-element.47), channel_id=1, source_target_pairs={{0,4},{4,0},{1,5},{5,1},{2,6},{6,2},{3,7},{7,3}} | collective-permute-start | bytes 23592968 | tf_op jit(solution)/shard_map/ppermute | solution.py:506
  802.6 389.5 %collective-permute-start.20 = (bf16[2048,2560]{1,0:T(8,128)(2,1)}, bf16[2048,2560]{1,0:T(8,128)(2,1)}, u32[]{:S(2)}, u32[]{:S(2)}) collective-permute-start(bf16[2048,2560]{1,0:T(8,128)(2,1)} %get-tuple-element.48), channel_id=1, source_target_pairs={{0,4},{4,0},{1,5},{5,1},{2,6},{6,2},{3,7},{7,3}} | collective-permute-start | bytes 31457288 | tf_op jit(solution)/shard_map/ppermute | solution.py:506
  809.3 130.2 %collective-permute-start.18 = (f32[512,2560]{1,0:T(8,128)}, f32[512,2560]{1,0:T(8,128)}, u32[]{:S(2)}, u32[]{:S(2)}) collective-permute-start(f32[512,2560]{1,0:T(8,128)} %add.19), channel_id=1, source_target_pairs={{0,2},{1,3},{2,0},{3,1},{4,6},{5,7},{6,4},{7,5}} | collective-permute-start | bytes 15728648 | tf_op jit(solution)/shard_map/ppermute | solution.py:502
  (9 other events, 222.6 us)
